TPU v7x, 256 devices: a whole 4x4x8 slice. The times are simulated.
256 devices in a mesh: lat: 8 (over z), lon: 16 (over x, y), obs: 2 (over core).
Axes of the slice: x: 4, y: 4, z: 8, core: 2. Of those that a mesh axis runs over, the one named last changes fastest.
Arguments:
- innovation: float32 [32768, 128], P(('lat', 'lon', 'obs')), may hold values from -6 to 6
- obs_error: float32 [32768, 128], P(('lat', 'lon', 'obs')), may hold values from 0.5 to 2
- obs_offset: float32 [2, 32768, 128], P(None, ('lat', 'lon', 'obs')), may hold values from 0 to 1
- obs_cell: int32 [32768, 128], P(('lat', 'lon', 'obs')), may hold values from 0 to 65535
- obs_owner: int32 [256, 128], P(('lat', 'lon', 'obs')), may hold values from 0 to 127, as said below
- block_count: int32 [256], P(('lat', 'lon', 'obs')), may hold values from 64 to 128
- land_mask: int32 [512, 16384], P(('lat', 'obs'), 'lon'), may hold values from 0 to 1, as said below
- inertia: float32 [512, 16384], P(('lat', 'obs'), 'lon'), may hold values from 0.002 to 0.05
- sea_depth: float32 [512, 16384], P(('lat', 'obs'), 'lon'), may hold values from 0.5 to 5
Outputs:
- adjoint_field: float32 [512, 16384], P(('lat', 'obs'), 'lon')
- residual: float32 [512, 16384], P(('lat', 'obs'), 'lon')
Inputs may be any that keep to these rules, and one draw needn't show every extreme that they name: `obs_owner`: among the live blocks of one device at most 3 name the same tile; in every draw some tile is named by exactly 3 live blocks of every device. `land_mask`: the first and the last grid row are land.
All inputs are finite; a program needn't handle non-finite values.
Results may differ from a plain program's by a relative error of at most 0.0003.
Values sent between devices are 32-bit elements; how exact they have to be, the bound alone decides.
No kernel may reach another device: no remote copies, remote signals or barrier semaphores. Data moves between devices by JAX's collectives and lax.ppermute only.
A program may use at most 64 MiB of HBM per device.

v0:
```python
import jax
import jax.numpy as jnp
from jax import lax
from jax.sharding import Mesh
from jax.sharding import PartitionSpec as P

ITERS = 5
LON = ("lon_0", "lon_1")
LAT_LON_OBS = ("lat", "lon_0", "lon_1", "obs")
LAT_LON = ("lat", "lon_0", "lon_1")


def extended(block, sides, width):
    for axis, dim in sides:
        count = lax.axis_size(axis)
        forward = [(i, i + 1) for i in range(count - 1)]
        forward.append((count - 1, 0))
        backward = [(target, source) for source, target in forward]
        low = lax.ppermute(
            lax.slice_in_dim(block, block.shape[dim] - width, None, axis=dim), axis, forward
        )
        high = lax.ppermute(lax.slice_in_dim(block, 0, width, axis=dim), axis, backward)
        block = jnp.concatenate([low, block, high], axis=dim)
    return block


def by_axis(value, axes):
    for axis in axes:
        value = lax.psum(value, axis)
    return value


def cut_along(value, dim, peers):
    shape = value.shape
    tiles = value.reshape(*shape[:dim], peers, shape[dim] // peers, *shape[dim + 1 :])
    return jnp.moveaxis(tiles, dim, 0)


def in_order(tiles, dim):
    tiles = jnp.moveaxis(tiles, 0, dim)
    shape = tiles.shape
    return tiles.reshape(*shape[:dim], shape[dim] * shape[dim + 1], *shape[dim + 2 :])


def exchange_both(value, axis, axes, splits, concats):
    sizes = [lax.axis_size(a) for a in axes]
    tiles = cut_along(value, splits[0], sizes[0])
    tiles = jnp.moveaxis(cut_along(tiles, splits[1] + 1, sizes[1]), 0, 1)
    inside = tiles.shape[2:]
    tiles = tiles.reshape(-1, *inside)
    tiles = lax.all_to_all(tiles, axis, split_axis=0, concat_axis=0, tiled=True)
    tiles = in_order(tiles.reshape(*sizes, *inside), concats[0] + 1)
    return in_order(tiles, concats[1])


def shifted(value, axis, steps):
    count = lax.axis_size(axis)
    pairs = [(source, (source + steps) % count) for source in range(count)]
    return lax.ppermute(value, axis, pairs)


def shifted_2(block, axis, distance):
    devices = range(lax.axis_size(axis))
    route = [(i - distance, i) for i in devices if i - distance in devices]
    return lax.ppermute(block, axis, route)


def sent_and_summed(value, axis, dim):
    tiles = cut_along(value, dim, lax.axis_size(axis))
    arrived = lax.all_to_all(tiles, axis, split_axis=0, concat_axis=0, tiled=True)
    return arrived.sum(axis=0)


def border(field):
    return extended(field, ((("lat", "obs"), 0), (LON, 1)), 1)


def two_products(residual, applied):
    return (
        by_axis(jnp.sum(residual * residual), LAT_LON_OBS),
        by_axis(jnp.sum(residual * applied), LAT_LON_OBS),
    )


def body(
    innovation,
    obs_error,
    obs_offset,
    obs_cell,
    obs_owner,
    block_count,
    land_mask,
    inertia,
    sea_depth,
):
    block_total = obs_owner.shape[1]
    block_width = innovation.shape[1]
    n_lat = lax.axis_size("lat")
    n_lon = lax.axis_size(LON)
    tile_count = n_lat * n_lon
    capacity = max(3, 2 * ((block_total + tile_count - 1) // tile_count))
    slot_total = tile_count * capacity
    tile_rows = land_mask.shape[0] * lax.axis_size("obs")
    tile_cols = land_mask.shape[1]
    owners = obs_owner[0]
    block_ids = jnp.arange(block_total)
    is_live = block_ids < block_count[0]
    earlier = block_ids[None, :] < block_ids[:, None]
    same_owner = (owners[None, :] == owners[:, None]) & earlier & is_live[None, :]
    slot_rank = jnp.sum(same_owner.astype(jnp.int32), axis=1)
    target = jnp.where(is_live, owners * capacity + slot_rank, slot_total)
    scaled = innovation / (obs_error * obs_error)
    floats = jnp.stack([scaled, obs_offset[0], obs_offset[1]], axis=1)

    def put_slots(values):
        holder = jnp.zeros((slot_total + 1,) + values.shape[1:], values.dtype)
        return holder.at[target].set(values)[:slot_total]

    sent_floats = put_slots(floats)
    sent_cells = put_slots(obs_cell)
    received, cell_ids = (
        exchange_both(
            sent_floats.reshape(n_lat, n_lon, capacity, 3, block_width),
            LAT_LON,
            ("lat", LON),
            (0, 1),
            (0, 1),
        ),
        exchange_both(
            sent_cells.reshape(n_lat, n_lon, capacity, block_width),
            LAT_LON,
            ("lat", LON),
            (0, 1),
            (0, 1),
        ),
    )
    received = received.reshape(-1, 3, block_width)
    cell_ids = cell_ids.reshape(-1, block_width)
    group = 1
    for size_try in range(1, slot_total + 1):
        if slot_total % size_try == 0 and size_try * block_width <= 4096:
            group = size_try
    turns = slot_total // group
    group_obs = group * block_width
    scaled_in = received[:, 0].reshape(turns, group_obs)
    north_frac = received[:, 1].reshape(turns, group_obs)
    east_frac = received[:, 2].reshape(turns, group_obs)
    cells_in = cell_ids.reshape(turns, group_obs)
    wide = tile_cols + 1
    row_axis = jnp.arange(tile_rows + 1, dtype=jnp.int32)[:, None]
    col_axis = jnp.arange(wide, dtype=jnp.int32)[None, :]

    def spread(total, pieces):
        amount, north, east, cells = pieces
        cell_row = (cells // tile_cols)[None, :]
        cell_col = (cells % tile_cols)[:, None]
        row_weights = (
            jnp.where(row_axis == cell_row, 1.0 - north[None, :], 0.0)
            + jnp.where(row_axis == cell_row + 1, north[None, :], 0.0)
        ) * amount[None, :]
        col_weights = jnp.where(col_axis == cell_col, 1.0 - east[:, None], 0.0) + jnp.where(
            col_axis == cell_col + 1, east[:, None], 0.0
        )
        return (
            total
            + jnp.dot(
                row_weights,
                col_weights,
                precision=lax.Precision.HIGHEST,
                preferred_element_type=jnp.float32,
            ),
            None,
        )

    partial_value, unused = lax.scan(
        spread,
        jnp.zeros((tile_rows + 1, wide), jnp.float32),
        (scaled_in, north_frac, east_frac, cells_in),
    )
    arrived_col = shifted(partial_value[:, tile_cols], LON, 1)
    partial_value = partial_value[:, :tile_cols].at[:, 0].add(arrived_col)
    arrived_row = shifted_2(partial_value[tile_rows], "lat", 1)
    tile_part = partial_value[:tile_rows].at[0].add(arrived_row)
    ocean = land_mask.astype(jnp.float32)
    forcing = sent_and_summed(tile_part, "obs", 0) * ocean
    conduct = ocean * sea_depth
    padded = border(conduct)
    cond_north = jnp.sqrt(conduct * padded[:-2, 1:-1])
    cond_south = jnp.sqrt(conduct * padded[2:, 1:-1])
    cond_west = jnp.sqrt(conduct * padded[1:-1, :-2])
    cond_east = jnp.sqrt(conduct * padded[1:-1, 2:])
    diagonal = inertia + cond_north + cond_south + cond_west + cond_east

    def operate(field):
        outer = border(field)
        return (
            diagonal * field
            - cond_north * outer[:-2, 1:-1]
            - cond_south * outer[2:, 1:-1]
            - cond_west * outer[1:-1, :-2]
            - cond_east * outer[1:-1, 2:]
        )

    adjoint_field = jnp.zeros_like(forcing)
    residual = forcing
    applied = operate(residual)
    norm_now, product = two_products(residual, applied)
    step_size = norm_now / product
    direction = residual
    applied_dir = applied
    for iteration in range(ITERS):
        adjoint_field = adjoint_field + step_size * direction
        residual = residual - step_size * applied_dir
        if iteration + 1 < ITERS:
            applied = operate(residual)
            norm_next, product = two_products(residual, applied)
            beta_ratio = norm_next / norm_now
            step_size = norm_next / (product - beta_ratio * norm_next / step_size)
            direction = residual + beta_ratio * direction
            applied_dir = applied + beta_ratio * applied_dir
            norm_now = norm_next
    return (adjoint_field, residual)


def solution(mesh):
    split = Mesh(
        mesh.devices.reshape(mesh.shape["lat"], 4, 4, mesh.shape["obs"]),
        ("lat", "lon_0", "lon_1", "obs"),
    )
    return jax.shard_map(
        body,
        mesh=split,
        in_specs=(
            P(LAT_LON_OBS, None),
            P(LAT_LON_OBS, None),
            P(None, LAT_LON_OBS, None),
            P(LAT_LON_OBS, None),
            P(LAT_LON_OBS, None),
            P(LAT_LON_OBS),
            P(("lat", "obs"), LON),
            P(("lat", "obs"), LON),
            P(("lat", "obs"), LON),
        ),
        out_specs=(P(("lat", "obs"), LON), P(("lat", "obs"), LON)),
        check_vma=False,
    )
```

profile of v0, /device:TPU:1, one launch (start us, length us, event | category | flops | bytes accessed | tf_op | source)
XLA Modules:
  0.0 609.3 jit_solution(17351134791260999394)
XLA Ops:
  4.8 16.3 %all-to-all-start = ((s32[128,1,1,3,128]{4,2,3,1,0:T(1,128)}), s32[128,1,1,3,128]{4,2,3,1,0:T(1,128)S(1)}, u32[]{:S(2)}, u32[]{:S(2)}) async-start(s32[128,1,1,3,128]{4,2,3,1,0:T(1,128)} %bitcast.5), calls=%async_computation | async-start | bytes 393216 | tf_op jit(solution)/shard_map/all_to_all | solution.py:51
  33.1 7.6 %all-to-all-start.1 = ((f32[128,1,1,3,3,128]{5,2,4,3,1,0:T(1,128)}), f32[128,1,1,3,3,128]{5,2,4,3,1,0:T(1,128)S(1)}, u32[]{:S(2)}, u32[]{:S(2)}) async-start(f32[128,1,1,3,3,128]{5,2,4,3,1,0:T(1,128)} %copy.29), calls=%async_computation.1 | async-start | bytes 1179648 | tf_op jit(solution)/shard_map/all_to_all | solution.py:51
  40.9 19.1 %all-to-all-done.1 = f32[128,1,1,3,3,128]{5,2,4,3,1,0:T(1,128)S(1)} async-done(((f32[128,1,1,3,3,128]{5,2,4,3,1,0:T(1,128)}), f32[128,1,1,3,3,128]{5,2,4,3,1,0:T(1,128)S(1)}, u32[]{:S(2)}, u32[]{:S(2)}) %all-to-all-start.1) | async-done | bytes 589856 | tf_op jit(solution)/shard_map/all_to_all | solution.py:51
  60.7 236.9 %while.16 = (s32[]{:T(128)}, f32[65,1025]{1,0:T(8,128)S(1)}, s32[12,4096]{1,0:T(8,128)S(1)}, f32[12,4096]{1,0:T(8,128)S(1)}, f32[12,4096]{1,0:T(8,128)S(1)}, /*index=5*/f32[12,4096]{1,0:T(8,128)S(1)}, s32[]{:T(128)}, s32[]{:T(128)}) while((s32[]{:T(128)}, f32[65,1025]{1,0:T(8,128)S(1)}, s32[12,4096]{1,0:T(8,128)S(1)}, ...), condition=%wide.region_4.5_spmd.clone.clone, body=%wide.region_3.4_spmd.clone.clone.sunk | while | flops 3297597440 | bytes 942707 | solution.py:175
  61.3 18.7 %fusion.98 = f32[65,1025]{1,0:T(8,128)S(1)} fusion(f32[4096]{0:T(1024)S(1)} %bitcast.80, s32[4096]{0:T(1024)S(1)} %get-tuple-element.342, f32[4096]{0:T(1024)S(1)} %broadcast_subtract_fusion.5, s32[4096]{0:T(1024)S(1)} %get-tuple-element.343, f32[4096]{0:T(1024)S(1)} %bitcast.87, f32[4096]{0:T(1024)S(1)} %bitcast.86, s32[4096]{0:T(1024)S(1)} %bitcast.88, ...), kind=kOutput, calls=%fused_computation.15.clone.1 | convolution fusion | flops 3297474560 | bytes 680457 | tf_op jit(solution)/shard_map/while/body/eval_jaxpr/dot_general | solution.py:166
  80.3 18.7 %fusion.98 = f32[65,1025]{1,0:T(8,128)S(1)} fusion(f32[4096]{0:T(1024)S(1)} %bitcast.80, s32[4096]{0:T(1024)S(1)} %get-tuple-element.342, f32[4096]{0:T(1024)S(1)} %broadcast_subtract_fusion.5, s32[4096]{0:T(1024)S(1)} %get-tuple-element.343, f32[4096]{0:T(1024)S(1)} %bitcast.87, f32[4096]{0:T(1024)S(1)} %bitcast.86, s32[4096]{0:T(1024)S(1)} %bitcast.88, ...), kind=kOutput, calls=%fused_computation.15.clone.1 | convolution fusion | flops 3297474560 | bytes 680457 | tf_op jit(solution)/shard_map/while/body/eval_jaxpr/dot_general | solution.py:166
  99.3 18.7 %fusion.98 = f32[65,1025]{1,0:T(8,128)S(1)} fusion(f32[4096]{0:T(1024)S(1)} %bitcast.80, s32[4096]{0:T(1024)S(1)} %get-tuple-element.342, f32[4096]{0:T(1024)S(1)} %broadcast_subtract_fusion.5, s32[4096]{0:T(1024)S(1)} %get-tuple-element.343, f32[4096]{0:T(1024)S(1)} %bitcast.87, f32[4096]{0:T(1024)S(1)} %bitcast.86, s32[4096]{0:T(1024)S(1)} %bitcast.88, ...), kind=kOutput, calls=%fused_computation.15.clone.1 | convolution fusion | flops 3297474560 | bytes 680457 | tf_op jit(solution)/shard_map/while/body/eval_jaxpr/dot_general | solution.py:166
  118.3 18.7 %fusion.98 = f32[65,1025]{1,0:T(8,128)S(1)} fusion(f32[4096]{0:T(1024)S(1)} %bitcast.80, s32[4096]{0:T(1024)S(1)} %get-tuple-element.342, f32[4096]{0:T(1024)S(1)} %broadcast_subtract_fusion.5, s32[4096]{0:T(1024)S(1)} %get-tuple-element.343, f32[4096]{0:T(1024)S(1)} %bitcast.87, f32[4096]{0:T(1024)S(1)} %bitcast.86, s32[4096]{0:T(1024)S(1)} %bitcast.88, ...), kind=kOutput, calls=%fused_computation.15.clone.1 | convolution fusion | flops 3297474560 | bytes 680457 | tf_op jit(solution)/shard_map/while/body/eval_jaxpr/dot_general | solution.py:166
  137.3 18.7 %fusion.98 = f32[65,1025]{1,0:T(8,128)S(1)} fusion(f32[4096]{0:T(1024)S(1)} %bitcast.80, s32[4096]{0:T(1024)S(1)} %get-tuple-element.342, f32[4096]{0:T(1024)S(1)} %broadcast_subtract_fusion.5, s32[4096]{0:T(1024)S(1)} %get-tuple-element.343, f32[4096]{0:T(1024)S(1)} %bitcast.87, f32[4096]{0:T(1024)S(1)} %bitcast.86, s32[4096]{0:T(1024)S(1)} %bitcast.88, ...), kind=kOutput, calls=%fused_computation.15.clone.1 | convolution fusion | flops 3297474560 | bytes 680457 | tf_op jit(solution)/shard_map/while/body/eval_jaxpr/dot_general | solution.py:166
  156.2 18.7 %fusion.98 = f32[65,1025]{1,0:T(8,128)S(1)} fusion(f32[4096]{0:T(1024)S(1)} %bitcast.80, s32[4096]{0:T(1024)S(1)} %get-tuple-element.342, f32[4096]{0:T(1024)S(1)} %broadcast_subtract_fusion.5, s32[4096]{0:T(1024)S(1)} %get-tuple-element.343, f32[4096]{0:T(1024)S(1)} %bitcast.87, f32[4096]{0:T(1024)S(1)} %bitcast.86, s32[4096]{0:T(1024)S(1)} %bitcast.88, ...), kind=kOutput, calls=%fused_computation.15.clone.1 | convolution fusion | flops 3297474560 | bytes 680457 | tf_op jit(solution)/shard_map/while/body/eval_jaxpr/dot_general | solution.py:166
  175.2 18.7 %fusion.98 = f32[65,1025]{1,0:T(8,128)S(1)} fusion(f32[4096]{0:T(1024)S(1)} %bitcast.80, s32[4096]{0:T(1024)S(1)} %get-tuple-element.342, f32[4096]{0:T(1024)S(1)} %broadcast_subtract_fusion.5, s32[4096]{0:T(1024)S(1)} %get-tuple-element.343, f32[4096]{0:T(1024)S(1)} %bitcast.87, f32[4096]{0:T(1024)S(1)} %bitcast.86, s32[4096]{0:T(1024)S(1)} %bitcast.88, ...), kind=kOutput, calls=%fused_computation.15.clone.1 | convolution fusion | flops 3297474560 | bytes 680457 | tf_op jit(solution)/shard_map/while/body/eval_jaxpr/dot_general | solution.py:166
  194.2 18.7 %fusion.98 = f32[65,1025]{1,0:T(8,128)S(1)} fusion(f32[4096]{0:T(1024)S(1)} %bitcast.80, s32[4096]{0:T(1024)S(1)} %get-tuple-element.342, f32[4096]{0:T(1024)S(1)} %broadcast_subtract_fusion.5, s32[4096]{0:T(1024)S(1)} %get-tuple-element.343, f32[4096]{0:T(1024)S(1)} %bitcast.87, f32[4096]{0:T(1024)S(1)} %bitcast.86, s32[4096]{0:T(1024)S(1)} %bitcast.88, ...), kind=kOutput, calls=%fused_computation.15.clone.1 | convolution fusion | flops 3297474560 | bytes 680457 | tf_op jit(solution)/shard_map/while/body/eval_jaxpr/dot_general | solution.py:166
  213.2 18.7 %fusion.98 = f32[65,1025]{1,0:T(8,128)S(1)} fusion(f32[4096]{0:T(1024)S(1)} %bitcast.80, s32[4096]{0:T(1024)S(1)} %get-tuple-element.342, f32[4096]{0:T(1024)S(1)} %broadcast_subtract_fusion.5, s32[4096]{0:T(1024)S(1)} %get-tuple-element.343, f32[4096]{0:T(1024)S(1)} %bitcast.87, f32[4096]{0:T(1024)S(1)} %bitcast.86, s32[4096]{0:T(1024)S(1)} %bitcast.88, ...), kind=kOutput, calls=%fused_computation.15.clone.1 | convolution fusion | flops 3297474560 | bytes 680457 | tf_op jit(solution)/shard_map/while/body/eval_jaxpr/dot_general | solution.py:166
  232.2 18.7 %fusion.98 = f32[65,1025]{1,0:T(8,128)S(1)} fusion(f32[4096]{0:T(1024)S(1)} %bitcast.80, s32[4096]{0:T(1024)S(1)} %get-tuple-element.342, f32[4096]{0:T(1024)S(1)} %broadcast_subtract_fusion.5, s32[4096]{0:T(1024)S(1)} %get-tuple-element.343, f32[4096]{0:T(1024)S(1)} %bitcast.87, f32[4096]{0:T(1024)S(1)} %bitcast.86, s32[4096]{0:T(1024)S(1)} %bitcast.88, ...), kind=kOutput, calls=%fused_computation.15.clone.1 | convolution fusion | flops 3297474560 | bytes 680457 | tf_op jit(solution)/shard_map/while/body/eval_jaxpr/dot_general | solution.py:166
  251.2 18.7 %fusion.98 = f32[65,1025]{1,0:T(8,128)S(1)} fusion(f32[4096]{0:T(1024)S(1)} %bitcast.80, s32[4096]{0:T(1024)S(1)} %get-tuple-element.342, f32[4096]{0:T(1024)S(1)} %broadcast_subtract_fusion.5, s32[4096]{0:T(1024)S(1)} %get-tuple-element.343, f32[4096]{0:T(1024)S(1)} %bitcast.87, f32[4096]{0:T(1024)S(1)} %bitcast.86, s32[4096]{0:T(1024)S(1)} %bitcast.88, ...), kind=kOutput, calls=%fused_computation.15.clone.1 | convolution fusion | flops 3297474560 | bytes 680457 | tf_op jit(solution)/shard_map/while/body/eval_jaxpr/dot_general | solution.py:166
  270.2 18.7 %fusion.98 = f32[65,1025]{1,0:T(8,128)S(1)} fusion(f32[4096]{0:T(1024)S(1)} %bitcast.80, s32[4096]{0:T(1024)S(1)} %get-tuple-element.342, f32[4096]{0:T(1024)S(1)} %broadcast_subtract_fusion.5, s32[4096]{0:T(1024)S(1)} %get-tuple-element.343, f32[4096]{0:T(1024)S(1)} %bitcast.87, f32[4096]{0:T(1024)S(1)} %bitcast.86, s32[4096]{0:T(1024)S(1)} %bitcast.88, ...), kind=kOutput, calls=%fused_computation.15.clone.1 | convolution fusion | flops 3297474560 | bytes 680457 | tf_op jit(solution)/shard_map/while/body/eval_jaxpr/dot_general | solution.py:166
  308.0 9.0 %all_to_all.15 = f32[2,32,1024]{2,1,0:T(8,128)S(1)} all-to-all(f32[2,32,1024]{2,1,0:T(8,128)S(1)} %bitcast.83), channel_id=1, replica_groups=mesh['lat'=8,'lon_0'=4,'lon_1'=4,'obs'=2] {'obs'}, dimensions={0} | all-to-all | bytes 524288 | tf_op jit(solution)/shard_map/all_to_all | solution.py:70
  334.3 13.2 %all-reduce.4 = (f32[]{:T(128)}, f32[]{:T(128)}) all-reduce(f32[]{:T(128)} %get-tuple-element.194, f32[]{:T(128)} %get-tuple-element.193), channel_id=1, replica_groups=mesh['lat'=8,'lon_0'=4,'lon_1'=4,'obs'=2] {'lat'}, use_global_device_ids=true, to_apply=%region_8.9 | all-reduce | flops 2 | bytes 16 | tf_op jit(solution)/shard_map/psum | solution.py:29
  354.1 11.7 %all-reduce.9 = (f32[]{:T(128)}, f32[]{:T(128)}) all-reduce(f32[]{:T(128)} %get-tuple-element.235, f32[]{:T(128)} %get-tuple-element.236), channel_id=1, replica_groups=mesh['lat'=8,'lon_0'=4,'lon_1'=4,'obs'=2] {'lon_1'}, use_global_device_ids=true, to_apply=%region_10.11 | all-reduce | flops 2 | bytes 16 | tf_op jit(solution)/shard_map/psum | solution.py:29
  365.7 11.4 %all-reduce.19 = (f32[]{:T(128)}, f32[]{:T(128)}) all-reduce(f32[]{:T(128)} %get-tuple-element.225, f32[]{:T(128)} %get-tuple-element.226), channel_id=1, replica_groups=mesh['lat'=8,'lon_0'=4,'lon_1'=4,'obs'=2] {'obs'}, use_global_device_ids=true, to_apply=%region_11.12 | all-reduce | flops 2 | bytes 16 | tf_op jit(solution)/shard_map/psum | solution.py:29
  390.9 13.4 %all-reduce.3 = (f32[]{:T(128)}, f32[]{:T(128)}) all-reduce(f32[]{:T(128)} %get-tuple-element.192, f32[]{:T(128)} %get-tuple-element.191), channel_id=1, replica_groups=mesh['lat'=8,'lon_0'=4,'lon_1'=4,'obs'=2] {'lat'}, use_global_device_ids=true, to_apply=%region_18.19 | all-reduce | flops 2 | bytes 16 | tf_op jit(solution)/shard_map/psum | solution.py:29
  411.0 11.9 %all-reduce.8 = (f32[]{:T(128)}, f32[]{:T(128)}) all-reduce(f32[]{:T(128)} %get-tuple-element.233, f32[]{:T(128)} %get-tuple-element.234), channel_id=1, replica_groups=mesh['lat'=8,'lon_0'=4,'lon_1'=4,'obs'=2] {'lon_1'}, use_global_device_ids=true, to_apply=%region_20.21 | all-reduce | flops 2 | bytes 16 | tf_op jit(solution)/shard_map/psum | solution.py:29
  422.9 9.6 %all-reduce.18 = (f32[]{:T(128)}, f32[]{:T(128)}) all-reduce(f32[]{:T(128)} %get-tuple-element.223, f32[]{:T(128)} %get-tuple-element.224), channel_id=1, replica_groups=mesh['lat'=8,'lon_0'=4,'lon_1'=4,'obs'=2] {'obs'}, use_global_device_ids=true, to_apply=%region_21.22 | all-reduce | flops 2 | bytes 16 | tf_op jit(solution)/shard_map/psum | solution.py:29
  448.3 14.4 %all-reduce.2 = (f32[]{:T(128)}, f32[]{:T(128)}) all-reduce(f32[]{:T(128)} %get-tuple-element.190, f32[]{:T(128)} %get-tuple-element.189), channel_id=1, replica_groups=mesh['lat'=8,'lon_0'=4,'lon_1'=4,'obs'=2] {'lat'}, use_global_device_ids=true, to_apply=%region_28.29 | all-reduce | flops 2 | bytes 16 | tf_op jit(solution)/shard_map/psum | solution.py:29
  469.3 11.9 %all-reduce.7 = (f32[]{:T(128)}, f32[]{:T(128)}) all-reduce(f32[]{:T(128)} %get-tuple-element.231, f32[]{:T(128)} %get-tuple-element.232), channel_id=1, replica_groups=mesh['lat'=8,'lon_0'=4,'lon_1'=4,'obs'=2] {'lon_1'}, use_global_device_ids=true, to_apply=%region_30.31 | all-reduce | flops 2 | bytes 16 | tf_op jit(solution)/shard_map/psum | solution.py:29
  481.2 8.8 %all-reduce.17 = (f32[]{:T(128)}, f32[]{:T(128)}) all-reduce(f32[]{:T(128)} %get-tuple-element.221, f32[]{:T(128)} %get-tuple-element.222), channel_id=1, replica_groups=mesh['lat'=8,'lon_0'=4,'lon_1'=4,'obs'=2] {'obs'}, use_global_device_ids=true, to_apply=%region_31.32 | all-reduce | flops 2 | bytes 16 | tf_op jit(solution)/shard_map/psum | solution.py:29
  506.4 13.4 %all-reduce.1 = (f32[]{:T(128)}, f32[]{:T(128)}) all-reduce(f32[]{:T(128)} %get-tuple-element.188, f32[]{:T(128)} %get-tuple-element.187), channel_id=1, replica_groups=mesh['lat'=8,'lon_0'=4,'lon_1'=4,'obs'=2] {'lat'}, use_global_device_ids=true, to_apply=%region_38.39 | all-reduce | flops 2 | bytes 16 | tf_op jit(solution)/shard_map/psum | solution.py:29
  526.3 11.9 %all-reduce.6 = (f32[]{:T(128)}, f32[]{:T(128)}) all-reduce(f32[]{:T(128)} %get-tuple-element.229, f32[]{:T(128)} %get-tuple-element.230), channel_id=1, replica_groups=mesh['lat'=8,'lon_0'=4,'lon_1'=4,'obs'=2] {'lon_1'}, use_global_device_ids=true, to_apply=%region_40.41 | all-reduce | flops 2 | bytes 16 | tf_op jit(solution)/shard_map/psum | solution.py:29
  538.2 9.5 %all-reduce.16 = (f32[]{:T(128)}, f32[]{:T(128)}) all-reduce(f32[]{:T(128)} %get-tuple-element.219, f32[]{:T(128)} %get-tuple-element.220), channel_id=1, replica_groups=mesh['lat'=8,'lon_0'=4,'lon_1'=4,'obs'=2] {'obs'}, use_global_device_ids=true, to_apply=%region_41.42 | all-reduce | flops 2 | bytes 16 | tf_op jit(solution)/shard_map/psum | solution.py:29
  562.8 14.4 %all-reduce = (f32[]{:T(128)}, f32[]{:T(128)}) all-reduce(f32[]{:T(128)} %get-tuple-element.186, f32[]{:T(128)} %get-tuple-element.185), channel_id=1, replica_groups=mesh['lat'=8,'lon_0'=4,'lon_1'=4,'obs'=2] {'lat'}, use_global_device_ids=true, to_apply=%region_48.49 | all-reduce | flops 2 | bytes 16 | tf_op jit(solution)/shard_map/psum | solution.py:29
  583.7 11.9 %all-reduce.5 = (f32[]{:T(128)}, f32[]{:T(128)}) all-reduce(f32[]{:T(128)} %get-tuple-element.227, f32[]{:T(128)} %get-tuple-element.228), channel_id=1, replica_groups=mesh['lat'=8,'lon_0'=4,'lon_1'=4,'obs'=2] {'lon_1'}, use_global_device_ids=true, to_apply=%region_50.51 | all-reduce | flops 2 | bytes 16 | tf_op jit(solution)/shard_map/psum | solution.py:29
  595.7 8.8 %all-reduce.15 = (f32[]{:T(128)}, f32[]{:T(128)}) all-reduce(f32[]{:T(128)} %get-tuple-element.217, f32[]{:T(128)} %get-tuple-element.218), channel_id=1, replica_groups=mesh['lat'=8,'lon_0'=4,'lon_1'=4,'obs'=2] {'obs'}, use_global_device_ids=true, to_apply=%region_51.52 | all-reduce | flops 2 | bytes 16 | tf_op jit(solution)/shard_map/psum | solution.py:29
  (187 shorter events, 127.0 us)
Async XLA Ops:
  0.6 20.5 %copy-start.3 = (f32[2,128,128]{2,1,0:T(8,128)S(1)}, f32[2,128,128]{2,1,0:T(8,128)}, u32[]{:S(2)}) copy-start(f32[2,128,128]{2,1,0:T(8,128)} %param.17) | copy-start | bytes 393220
  0.6 20.6 %copy-start.4 = (f32[128,128]{1,0:T(8,128)S(1)}, f32[128,128]{1,0:T(8,128)}, u32[]{:S(2)}) copy-start(f32[128,128]{1,0:T(8,128)} %param.15) | copy-start | bytes 196612
  0.7 20.6 %copy-start.5 = (f32[128,128]{1,0:T(8,128)S(1)}, f32[128,128]{1,0:T(8,128)}, u32[]{:S(2)}) copy-start(f32[128,128]{1,0:T(8,128)} %param.16) | copy-start | bytes 196612
  4.8 28.3 %all-to-all-start = ((s32[128,1,1,3,128]{4,2,3,1,0:T(1,128)}), s32[128,1,1,3,128]{4,2,3,1,0:T(1,128)S(1)}, u32[]{:S(2)}, u32[]{:S(2)}) async-start(s32[128,1,1,3,128]{4,2,3,1,0:T(1,128)} %bitcast.5), calls=%async_computation | async-start | bytes 393216 | tf_op jit(solution)/shard_map/all_to_all | solution.py:51
  33.1 26.9 %all-to-all-start.1 = ((f32[128,1,1,3,3,128]{5,2,4,3,1,0:T(1,128)}), f32[128,1,1,3,3,128]{5,2,4,3,1,0:T(1,128)S(1)}, u32[]{:S(2)}, u32[]{:S(2)}) async-start(f32[128,1,1,3,3,128]{5,2,4,3,1,0:T(1,128)} %copy.29), calls=%async_computation.1 | async-start | bytes 1179648 | tf_op jit(solution)/shard_map/all_to_all | solution.py:51
  297.7 5.8 collective-permute-start
  304.5 3.4 collective-permute-start.1
  317.0 16.3 %copy-start = (f32[32,1024]{1,0:T(8,128)S(1)}, f32[32,1024]{1,0:T(8,128)}, u32[]{:S(2)}) copy-start(f32[32,1024]{1,0:T(8,128)} %param.22) | copy-start | bytes 393220
  317.1 4.0 collective-permute-start.2
  319.4 3.0 collective-permute-start.3
  319.4 7.9 %collective-permute-start.6 = (f32[1,1024]{1,0:T(1,128)S(1)}, f32[1,1024]{1,0:T(1,128)S(1)}, u32[]{:S(2)}, u32[]{:S(2)}) collective-permute-start(f32[1,1024]{1,0:T(1,128)S(1)} %get-tuple-element.291), channel_id=1, source_target_pairs={{0,1},{1,32},{32,33},{33,64},{64,65},{65,96},{96,97},{97,128},{128... | collective-permute-start | bytes 12296 | tf_op jit(solution)/shard_map/ppermute | solution.py:19
  321.1 6.2 %collective-permute-start.7 = (f32[1,1024]{1,0:T(1,128)S(1)}, f32[1,1024]{1,0:T(1,128)S(1)}, u32[]{:S(2)}, u32[]{:S(2)}) collective-permute-start(f32[1,1024]{1,0:T(1,128)S(1)} %get-tuple-element.292), channel_id=1, source_target_pairs={{1,0},{32,1},{33,32},{64,33},{65,64},{96,65},{97,96},{128,97},{129... | collective-permute-start | bytes 12296 | tf_op jit(solution)/shard_map/ppermute | solution.py:22
  322.5 9.7 %collective-permute-start.4 = (f32[34,1]{1,0:T(8,128)S(1)}, f32[34,1]{1,0:T(8,128)S(1)}, u32[]{:S(2)}, u32[]{:S(2)}) collective-permute-start(f32[34,1]{1,0:T(8,128)S(1)} %get-tuple-element.273), channel_id=1, source_target_pairs={{0,2},{2,4},{4,6},{6,8},{8,10},{10,12},{12,14},{14,16},{16,18},{18... | collective-permute-start | bytes 416 | tf_op jit(solution)/shard_map/ppermute | solution.py:19
  322.5 9.7 %collective-permute-start.5 = (f32[34,1]{1,0:T(8,128)S(1)}, f32[34,1]{1,0:T(8,128)S(1)}, u32[]{:S(2)}, u32[]{:S(2)}) collective-permute-start(f32[34,1]{1,0:T(8,128)S(1)} %get-tuple-element.274), channel_id=1, source_target_pairs={{2,0},{4,2},{6,4},{8,6},{10,8},{12,10},{14,12},{16,14},{18,16},{20... | collective-permute-start | bytes 416 | tf_op jit(solution)/shard_map/ppermute | solution.py:22
  327.4 6.0 collective-permute-start.8
  327.4 5.9 collective-permute-start.9
  378.5 2.7 collective-permute-start.10
  380.5 3.0 collective-permute-start.11
  383.6 6.4 %collective-permute-start.12 = (f32[34,1]{1,0:T(8,128)S(1)}, f32[34,1]{1,0:T(8,128)S(1)}, u32[]{:S(2)}, u32[]{:S(2)}) collective-permute-start(f32[34,1]{1,0:T(8,128)S(1)} %get-tuple-element.271), channel_id=1, source_target_pairs={{0,2},{2,4},{4,6},{6,8},{8,10},{10,12},{12,14},{14,16},{16,18},{18... | collective-permute-start | bytes 416 | tf_op jit(solution)/shard_map/ppermute | solution.py:19
  383.6 6.4 %collective-permute-start.13 = (f32[34,1]{1,0:T(8,128)S(1)}, f32[34,1]{1,0:T(8,128)S(1)}, u32[]{:S(2)}, u32[]{:S(2)}) collective-permute-start(f32[34,1]{1,0:T(8,128)S(1)} %get-tuple-element.272), channel_id=1, source_target_pairs={{2,0},{4,2},{6,4},{8,6},{10,8},{12,10},{14,12},{16,14},{18,16},{20... | collective-permute-start | bytes 416 | tf_op jit(solution)/shard_map/ppermute | solution.py:22
  437.1 1.9 collective-permute-start.14
  438.3 3.0 collective-permute-start.15
  441.4 6.0 collective-permute-start.16
  441.4 5.9 collective-permute-start.17
  494.0 2.7 collective-permute-start.18
  496.0 3.0 collective-permute-start.19
  499.1 6.4 %collective-permute-start.20 = (f32[34,1]{1,0:T(8,128)S(1)}, f32[34,1]{1,0:T(8,128)S(1)}, u32[]{:S(2)}, u32[]{:S(2)}) collective-permute-start(f32[34,1]{1,0:T(8,128)S(1)} %get-tuple-element.267), channel_id=1, source_target_pairs={{0,2},{2,4},{4,6},{6,8},{8,10},{10,12},{12,14},{14,16},{16,18},{18... | collective-permute-start | bytes 416 | tf_op jit(solution)/shard_map/ppermute | solution.py:19
  499.1 6.3 %collective-permute-start.21 = (f32[34,1]{1,0:T(8,128)S(1)}, f32[34,1]{1,0:T(8,128)S(1)}, u32[]{:S(2)}, u32[]{:S(2)}) collective-permute-start(f32[34,1]{1,0:T(8,128)S(1)} %get-tuple-element.268), channel_id=1, source_target_pairs={{2,0},{4,2},{6,4},{8,6},{10,8},{12,10},{14,12},{16,14},{18,16},{20... | collective-permute-start | bytes 416 | tf_op jit(solution)/shard_map/ppermute | solution.py:22
  551.6 1.9 collective-permute-start.22
  552.7 3.0 collective-permute-start.23
  555.9 6.0 collective-permute-start.24
  555.9 5.9 collective-permute-start.25
  (2 other events, 25.8 us)
where the time goes:
time: 615 us; the launch traced here: 609 us
  matrix products  225 us (37%)
  blocking collectives  218 us (35%)
  starting transfers between devices  66.1 us (11%)
  waiting for transfers between devices  50 us (8%)
  between operations  19.4 us (3%)
  other arithmetic  10.9 us (2%)
  local copies, waits for them, and re-layouts  10 us (2%)
  loops' own time  9.79 us (2%)
    dot_general x12, matrix products, spread(): jnp.dot(row_weights, col_weights, precision=lax.Precision.HIGHEST, prefer...  225 us
    psum x20, blocking collectives, by_axis(): value = lax.psum(value, axis)  209 us
    ppermute x12, starting transfers between devices, extended(): lax.ppermute(lax.slice_in_dim(block, 0, width, axis=dim), axis, backward)  28.7 us
    all_to_all x2, waiting for transfers between devices, exchange_both(): tiles = lax.all_to_all(tiles, axis, split_axis=0, concat_axis=0, tiled=True)  24.7 us
    all_to_all x2, starting transfers between devices, exchange_both(): tiles = lax.all_to_all(tiles, axis, split_axis=0, concat_axis=0, tiled=True)  23.9 us
  transfers between devices with their start and end apart: 28, of which 18 were waited for; matrix products, arithmetic and copies ran while one was open for 1% of the time, Pallas kernels for 0%

commit v1 on v0

--- a/solution.py
+++ b/solution.py
@@ -26,7 +26,7 @@
 
 def by_axis(value, axes):
     for axis in axes:
-        value = lax.psum(value, axis)
+        value = jnp.sum(jax.lax.all_gather(value, axis), axis=0)
     return value
 
 

time: 615 us -> 677 us (1.10)
  local copies, waits for them, and re-layouts: 10 us -> 67.4 us
  other arithmetic: 10.9 us -> 35.9 us
  blocking collectives: 218 us -> 205 us
  loops' own time: 9.79 us -> 1.43 us
    psum x20 -> x0, blocking collectives: 209 us -> none  [by_axis(): value = lax.psum(value, axis)]
    unnamed x0 -> x20, blocking collectives: none -> 196 us
    unnamed x12 -> x104, local copies, waits for them, and re-layouts: 0.03 us -> 57.4 us
    reduce_sum x0 -> x40, other arithmetic: none -> 24.9 us  [by_axis(): value = jnp.sum(jax.lax.all_gather(value, axis), axis=0)]
    another operation x1, loops' own time: 9.79 us -> 1.43 us  [body(): lax.scan(spread, jnp.zeros((tile_rows + 1, wide), jnp.float32), (scaled_i...]
  transfers between devices with their start and end apart: 28 -> 28, of which waited for: 18 -> 17; matrix products, arithmetic and copies ran while one was open for 1% -> 1% of each run, Pallas kernels for 0% -> 0%
where the time goes in v1:
time: 677 us; the launch traced here: 670 us
  matrix products  225 us (33%)
  blocking collectives  205 us (30%)
  local copies, waits for them, and re-layouts  67.4 us (10%)
  starting transfers between devices  66.3 us (10%)
  waiting for transfers between devices  49.1 us (7%)
  other arithmetic  35.9 us (5%)
  between operations  19.7 us (3%)
    dot_general x12, matrix products, spread(): jnp.dot(row_weights, col_weights, precision=lax.Precision.HIGHEST, prefer...  225 us
    unnamed x20, blocking collectives  196 us
    unnamed x104, local copies, waits for them, and re-layouts  57.4 us
    ppermute x12, starting transfers between devices, extended(): lax.ppermute(lax.slice_in_dim(block, 0, width, axis=dim), axis, backward)  28.8 us
    reduce_sum x40, other arithmetic, by_axis(): value = jnp.sum(jax.lax.all_gather(value, axis), axis=0)  24.9 us
    all_to_all x2, waiting for transfers between devices, exchange_both(): tiles = lax.all_to_all(tiles, axis, split_axis=0, concat_axis=0, tiled=True)  24.7 us
    all_to_all x2, starting transfers between devices, exchange_both(): tiles = lax.all_to_all(tiles, axis, split_axis=0, concat_axis=0, tiled=True)  23.9 us
  transfers between devices with their start and end apart: 28, of which 17 were waited for; matrix products, arithmetic and copies ran while one was open for 1% of the time, Pallas kernels for 0%

profile of v1, /device:TPU:1, one launch (start us, length us, event | category | flops | bytes accessed | tf_op | source)
XLA Modules:
  0.0 670.1 jit_solution(9589041479711257441)
XLA Ops:
  4.8 16.3 %all-to-all-start = ((s32[128,1,1,3,128]{4,2,3,1,0:T(1,128)}), s32[128,1,1,3,128]{4,2,3,1,0:T(1,128)S(1)}, u32[]{:S(2)}, u32[]{:S(2)}) async-start(s32[128,1,1,3,128]{4,2,3,1,0:T(1,128)} %bitcast.5), calls=%async_computation | async-start | bytes 393216 | tf_op jit(solution)/shard_map/all_to_all | solution.py:51
  33.1 7.6 %all-to-all-start.1 = ((f32[128,1,1,3,3,128]{5,2,4,3,1,0:T(1,128)}), f32[128,1,1,3,3,128]{5,2,4,3,1,0:T(1,128)S(1)}, u32[]{:S(2)}, u32[]{:S(2)}) async-start(f32[128,1,1,3,3,128]{5,2,4,3,1,0:T(1,128)} %copy.29), calls=%async_computation.1 | async-start | bytes 1179648 | tf_op jit(solution)/shard_map/all_to_all | solution.py:51
  40.9 19.1 %all-to-all-done.1 = f32[128,1,1,3,3,128]{5,2,4,3,1,0:T(1,128)S(1)} async-done(((f32[128,1,1,3,3,128]{5,2,4,3,1,0:T(1,128)}), f32[128,1,1,3,3,128]{5,2,4,3,1,0:T(1,128)S(1)}, u32[]{:S(2)}, u32[]{:S(2)}) %all-to-all-start.1) | async-done | bytes 589856 | tf_op jit(solution)/shard_map/all_to_all | solution.py:51
  60.7 228.5 %while.16 = (s32[]{:T(128)}, f32[65,1025]{1,0:T(8,128)S(1)}, s32[12,4096]{1,0:T(8,128)S(1)}, f32[12,4096]{1,0:T(8,128)S(1)}, f32[12,4096]{1,0:T(8,128)S(1)}, /*index=5*/f32[12,4096]{1,0:T(8,128)S(1)}, s32[]{:T(128)}, s32[]{:T(128)}) while((s32[]{:T(128)}, f32[65,1025]{1,0:T(8,128)S(1)}, s32[12,4096]{1,0:T(8,128)S(1)}, ...), condition=%wide.region_4.5_spmd.clone.clone, body=%wide.region_3.4_spmd.clone.clone.sunk | while | flops 3297597440 | bytes 942707 | solution.py:175
  61.4 18.7 %fusion.98 = f32[65,1025]{1,0:T(8,128)S(1)} fusion(f32[4096]{0:T(1024)S(1)} %bitcast.124, s32[4096]{0:T(1024)S(1)} %get-tuple-element.342, f32[4096]{0:T(1024)S(1)} %broadcast_subtract_fusion.5, s32[4096]{0:T(1024)S(1)} %get-tuple-element.343, f32[4096]{0:T(1024)S(1)} %bitcast.131, f32[4096]{0:T(1024)S(1)} %bitcast.130, s32[4096]{0:T(1024)S(1)} %bitcast.132, ...), kind=kOutput, calls=%fused_computation.15.clone.1 | convolution fusion | flops 3297474560 | bytes 680457 | tf_op jit(solution)/shard_map/while/body/eval_jaxpr/dot_general | solution.py:166
  80.4 18.7 %fusion.98 = f32[65,1025]{1,0:T(8,128)S(1)} fusion(f32[4096]{0:T(1024)S(1)} %bitcast.124, s32[4096]{0:T(1024)S(1)} %get-tuple-element.342, f32[4096]{0:T(1024)S(1)} %broadcast_subtract_fusion.5, s32[4096]{0:T(1024)S(1)} %get-tuple-element.343, f32[4096]{0:T(1024)S(1)} %bitcast.131, f32[4096]{0:T(1024)S(1)} %bitcast.130, s32[4096]{0:T(1024)S(1)} %bitcast.132, ...), kind=kOutput, calls=%fused_computation.15.clone.1 | convolution fusion | flops 3297474560 | bytes 680457 | tf_op jit(solution)/shard_map/while/body/eval_jaxpr/dot_general | solution.py:166
  99.4 18.7 %fusion.98 = f32[65,1025]{1,0:T(8,128)S(1)} fusion(f32[4096]{0:T(1024)S(1)} %bitcast.124, s32[4096]{0:T(1024)S(1)} %get-tuple-element.342, f32[4096]{0:T(1024)S(1)} %broadcast_subtract_fusion.5, s32[4096]{0:T(1024)S(1)} %get-tuple-element.343, f32[4096]{0:T(1024)S(1)} %bitcast.131, f32[4096]{0:T(1024)S(1)} %bitcast.130, s32[4096]{0:T(1024)S(1)} %bitcast.132, ...), kind=kOutput, calls=%fused_computation.15.clone.1 | convolution fusion | flops 3297474560 | bytes 680457 | tf_op jit(solution)/shard_map/while/body/eval_jaxpr/dot_general | solution.py:166
  118.3 18.7 %fusion.98 = f32[65,1025]{1,0:T(8,128)S(1)} fusion(f32[4096]{0:T(1024)S(1)} %bitcast.124, s32[4096]{0:T(1024)S(1)} %get-tuple-element.342, f32[4096]{0:T(1024)S(1)} %broadcast_subtract_fusion.5, s32[4096]{0:T(1024)S(1)} %get-tuple-element.343, f32[4096]{0:T(1024)S(1)} %bitcast.131, f32[4096]{0:T(1024)S(1)} %bitcast.130, s32[4096]{0:T(1024)S(1)} %bitcast.132, ...), kind=kOutput, calls=%fused_computation.15.clone.1 | convolution fusion | flops 3297474560 | bytes 680457 | tf_op jit(solution)/shard_map/while/body/eval_jaxpr/dot_general | solution.py:166
  137.3 18.7 %fusion.98 = f32[65,1025]{1,0:T(8,128)S(1)} fusion(f32[4096]{0:T(1024)S(1)} %bitcast.124, s32[4096]{0:T(1024)S(1)} %get-tuple-element.342, f32[4096]{0:T(1024)S(1)} %broadcast_subtract_fusion.5, s32[4096]{0:T(1024)S(1)} %get-tuple-element.343, f32[4096]{0:T(1024)S(1)} %bitcast.131, f32[4096]{0:T(1024)S(1)} %bitcast.130, s32[4096]{0:T(1024)S(1)} %bitcast.132, ...), kind=kOutput, calls=%fused_computation.15.clone.1 | convolution fusion | flops 3297474560 | bytes 680457 | tf_op jit(solution)/shard_map/while/body/eval_jaxpr/dot_general | solution.py:166
  156.3 18.7 %fusion.98 = f32[65,1025]{1,0:T(8,128)S(1)} fusion(f32[4096]{0:T(1024)S(1)} %bitcast.124, s32[4096]{0:T(1024)S(1)} %get-tuple-element.342, f32[4096]{0:T(1024)S(1)} %broadcast_subtract_fusion.5, s32[4096]{0:T(1024)S(1)} %get-tuple-element.343, f32[4096]{0:T(1024)S(1)} %bitcast.131, f32[4096]{0:T(1024)S(1)} %bitcast.130, s32[4096]{0:T(1024)S(1)} %bitcast.132, ...), kind=kOutput, calls=%fused_computation.15.clone.1 | convolution fusion | flops 3297474560 | bytes 680457 | tf_op jit(solution)/shard_map/while/body/eval_jaxpr/dot_general | solution.py:166
  175.3 18.7 %fusion.98 = f32[65,1025]{1,0:T(8,128)S(1)} fusion(f32[4096]{0:T(1024)S(1)} %bitcast.124, s32[4096]{0:T(1024)S(1)} %get-tuple-element.342, f32[4096]{0:T(1024)S(1)} %broadcast_subtract_fusion.5, s32[4096]{0:T(1024)S(1)} %get-tuple-element.343, f32[4096]{0:T(1024)S(1)} %bitcast.131, f32[4096]{0:T(1024)S(1)} %bitcast.130, s32[4096]{0:T(1024)S(1)} %bitcast.132, ...), kind=kOutput, calls=%fused_computation.15.clone.1 | convolution fusion | flops 3297474560 | bytes 680457 | tf_op jit(solution)/shard_map/while/body/eval_jaxpr/dot_general | solution.py:166
  194.3 18.7 %fusion.98 = f32[65,1025]{1,0:T(8,128)S(1)} fusion(f32[4096]{0:T(1024)S(1)} %bitcast.124, s32[4096]{0:T(1024)S(1)} %get-tuple-element.342, f32[4096]{0:T(1024)S(1)} %broadcast_subtract_fusion.5, s32[4096]{0:T(1024)S(1)} %get-tuple-element.343, f32[4096]{0:T(1024)S(1)} %bitcast.131, f32[4096]{0:T(1024)S(1)} %bitcast.130, s32[4096]{0:T(1024)S(1)} %bitcast.132, ...), kind=kOutput, calls=%fused_computation.15.clone.1 | convolution fusion | flops 3297474560 | bytes 680457 | tf_op jit(solution)/shard_map/while/body/eval_jaxpr/dot_general | solution.py:166
  213.3 18.7 %fusion.98 = f32[65,1025]{1,0:T(8,128)S(1)} fusion(f32[4096]{0:T(1024)S(1)} %bitcast.124, s32[4096]{0:T(1024)S(1)} %get-tuple-element.342, f32[4096]{0:T(1024)S(1)} %broadcast_subtract_fusion.5, s32[4096]{0:T(1024)S(1)} %get-tuple-element.343, f32[4096]{0:T(1024)S(1)} %bitcast.131, f32[4096]{0:T(1024)S(1)} %bitcast.130, s32[4096]{0:T(1024)S(1)} %bitcast.132, ...), kind=kOutput, calls=%fused_computation.15.clone.1 | convolution fusion | flops 3297474560 | bytes 680457 | tf_op jit(solution)/shard_map/while/body/eval_jaxpr/dot_general | solution.py:166
  232.3 18.7 %fusion.98 = f32[65,1025]{1,0:T(8,128)S(1)} fusion(f32[4096]{0:T(1024)S(1)} %bitcast.124, s32[4096]{0:T(1024)S(1)} %get-tuple-element.342, f32[4096]{0:T(1024)S(1)} %broadcast_subtract_fusion.5, s32[4096]{0:T(1024)S(1)} %get-tuple-element.343, f32[4096]{0:T(1024)S(1)} %bitcast.131, f32[4096]{0:T(1024)S(1)} %bitcast.130, s32[4096]{0:T(1024)S(1)} %bitcast.132, ...), kind=kOutput, calls=%fused_computation.15.clone.1 | convolution fusion | flops 3297474560 | bytes 680457 | tf_op jit(solution)/shard_map/while/body/eval_jaxpr/dot_general | solution.py:166
  251.3 18.7 %fusion.98 = f32[65,1025]{1,0:T(8,128)S(1)} fusion(f32[4096]{0:T(1024)S(1)} %bitcast.124, s32[4096]{0:T(1024)S(1)} %get-tuple-element.342, f32[4096]{0:T(1024)S(1)} %broadcast_subtract_fusion.5, s32[4096]{0:T(1024)S(1)} %get-tuple-element.343, f32[4096]{0:T(1024)S(1)} %bitcast.131, f32[4096]{0:T(1024)S(1)} %bitcast.130, s32[4096]{0:T(1024)S(1)} %bitcast.132, ...), kind=kOutput, calls=%fused_computation.15.clone.1 | convolution fusion | flops 3297474560 | bytes 680457 | tf_op jit(solution)/shard_map/while/body/eval_jaxpr/dot_general | solution.py:166
  270.3 18.7 %fusion.98 = f32[65,1025]{1,0:T(8,128)S(1)} fusion(f32[4096]{0:T(1024)S(1)} %bitcast.124, s32[4096]{0:T(1024)S(1)} %get-tuple-element.342, f32[4096]{0:T(1024)S(1)} %broadcast_subtract_fusion.5, s32[4096]{0:T(1024)S(1)} %get-tuple-element.343, f32[4096]{0:T(1024)S(1)} %bitcast.131, f32[4096]{0:T(1024)S(1)} %bitcast.130, s32[4096]{0:T(1024)S(1)} %bitcast.132, ...), kind=kOutput, calls=%fused_computation.15.clone.1 | convolution fusion | flops 3297474560 | bytes 680457 | tf_op jit(solution)/shard_map/while/body/eval_jaxpr/dot_general | solution.py:166
  299.6 9.0 %all_to_all.15 = f32[2,32,1024]{2,1,0:T(8,128)S(1)} all-to-all(f32[2,32,1024]{2,1,0:T(8,128)S(1)} %bitcast.127), channel_id=1, replica_groups=mesh['lat'=8,'lon_0'=4,'lon_1'=4,'obs'=2] {'obs'}, dimensions={0} | all-to-all | bytes 524288 | tf_op jit(solution)/shard_map/all_to_all | solution.py:70
  329.4 12.5 %all-reduce.44 = (f32[8]{0:T(128)S(1)}, f32[8]{0:T(128)S(1)}) all-reduce(f32[8]{0:T(128)S(1)} %dynamic-update-slice.6, f32[8]{0:T(128)S(1)} %dynamic-update-slice.10), channel_id=1, replica_groups=mesh['lat'=8,'lon_0'=4,'lon_1'=4,'obs'=2] {'lat'}, use_global_device_ids=true, to_apply=%add | all-reduce | flops 16 | bytes 128
  356.9 11.0 %all-reduce.49 = (f32[4]{0:T(128)S(1)}, f32[4]{0:T(128)S(1)}) all-reduce(f32[4]{0:T(128)S(1)} %dynamic-update-slice.8, f32[4]{0:T(128)S(1)} %dynamic-update-slice.12), channel_id=1, replica_groups=mesh['lat'=8,'lon_0'=4,'lon_1'=4,'obs'=2] {'lon_1'}, use_global_device_ids=true, to_apply=%add.2 | all-reduce | flops 8 | bytes 64
  371.9 10.8 %all-reduce.59 = (f32[2]{0:T(128)S(1)}, f32[2]{0:T(128)S(1)}) all-reduce(f32[2]{0:T(128)S(1)} %dynamic-update-slice.9, f32[2]{0:T(128)S(1)} %dynamic-update-slice.13), channel_id=1, replica_groups=mesh['lat'=8,'lon_0'=4,'lon_1'=4,'obs'=2] {'obs'}, use_global_device_ids=true, to_apply=%add.3 | all-reduce | flops 4 | bytes 32
  400.6 12.6 %all-reduce.43 = (f32[8]{0:T(128)S(1)}, f32[8]{0:T(128)S(1)}) all-reduce(f32[8]{0:T(128)S(1)} %dynamic-update-slice.14, f32[8]{0:T(128)S(1)} %dynamic-update-slice.18), channel_id=1, replica_groups=mesh['lat'=8,'lon_0'=4,'lon_1'=4,'obs'=2] {'lat'}, use_global_device_ids=true, to_apply=%add.8 | all-reduce | flops 16 | bytes 128
  427.0 11.2 %all-reduce.48 = (f32[4]{0:T(128)S(1)}, f32[4]{0:T(128)S(1)}) all-reduce(f32[4]{0:T(128)S(1)} %dynamic-update-slice.16, f32[4]{0:T(128)S(1)} %dynamic-update-slice.20), channel_id=1, replica_groups=mesh['lat'=8,'lon_0'=4,'lon_1'=4,'obs'=2] {'lon_1'}, use_global_device_ids=true, to_apply=%add.10 | all-reduce | flops 8 | bytes 64
  442.1 8.9 %all-reduce.58 = (f32[2]{0:T(128)S(1)}, f32[2]{0:T(128)S(1)}) all-reduce(f32[2]{0:T(128)S(1)} %dynamic-update-slice.17, f32[2]{0:T(128)S(1)} %dynamic-update-slice.21), channel_id=1, replica_groups=mesh['lat'=8,'lon_0'=4,'lon_1'=4,'obs'=2] {'obs'}, use_global_device_ids=true, to_apply=%add.11 | all-reduce | flops 4 | bytes 32
  471.0 13.7 %all-reduce.42 = (f32[8]{0:T(128)S(1)}, f32[8]{0:T(128)S(1)}) all-reduce(f32[8]{0:T(128)S(1)} %dynamic-update-slice.22, f32[8]{0:T(128)S(1)} %dynamic-update-slice.26), channel_id=1, replica_groups=mesh['lat'=8,'lon_0'=4,'lon_1'=4,'obs'=2] {'lat'}, use_global_device_ids=true, to_apply=%add.16 | all-reduce | flops 16 | bytes 128
  498.5 11.5 %all-reduce.47 = (f32[4]{0:T(128)S(1)}, f32[4]{0:T(128)S(1)}) all-reduce(f32[4]{0:T(128)S(1)} %dynamic-update-slice.24, f32[4]{0:T(128)S(1)} %dynamic-update-slice.28), channel_id=1, replica_groups=mesh['lat'=8,'lon_0'=4,'lon_1'=4,'obs'=2] {'lon_1'}, use_global_device_ids=true, to_apply=%add.18 | all-reduce | flops 8 | bytes 64
  514.0 8.2 %all-reduce.57 = (f32[2]{0:T(128)S(1)}, f32[2]{0:T(128)S(1)}) all-reduce(f32[2]{0:T(128)S(1)} %dynamic-update-slice.25, f32[2]{0:T(128)S(1)} %dynamic-update-slice.29), channel_id=1, replica_groups=mesh['lat'=8,'lon_0'=4,'lon_1'=4,'obs'=2] {'obs'}, use_global_device_ids=true, to_apply=%add.19 | all-reduce | flops 4 | bytes 32
  542.6 12.7 %all-reduce.41 = (f32[8]{0:T(128)S(1)}, f32[8]{0:T(128)S(1)}) all-reduce(f32[8]{0:T(128)S(1)} %dynamic-update-slice.30, f32[8]{0:T(128)S(1)} %dynamic-update-slice.34), channel_id=1, replica_groups=mesh['lat'=8,'lon_0'=4,'lon_1'=4,'obs'=2] {'lat'}, use_global_device_ids=true, to_apply=%add.24 | all-reduce | flops 16 | bytes 128
  569.3 11.3 %all-reduce.46 = (f32[4]{0:T(128)S(1)}, f32[4]{0:T(128)S(1)}) all-reduce(f32[4]{0:T(128)S(1)} %dynamic-update-slice.32, f32[4]{0:T(128)S(1)} %dynamic-update-slice.36), channel_id=1, replica_groups=mesh['lat'=8,'lon_0'=4,'lon_1'=4,'obs'=2] {'lon_1'}, use_global_device_ids=true, to_apply=%add.26 | all-reduce | flops 8 | bytes 64
  584.7 8.8 %all-reduce.56 = (f32[2]{0:T(128)S(1)}, f32[2]{0:T(128)S(1)}) all-reduce(f32[2]{0:T(128)S(1)} %dynamic-update-slice.33, f32[2]{0:T(128)S(1)} %dynamic-update-slice.37), channel_id=1, replica_groups=mesh['lat'=8,'lon_0'=4,'lon_1'=4,'obs'=2] {'obs'}, use_global_device_ids=true, to_apply=%add.27 | all-reduce | flops 4 | bytes 32
  612.9 13.6 %all-reduce.40 = (f32[8]{0:T(128)S(1)}, f32[8]{0:T(128)S(1)}) all-reduce(f32[8]{0:T(128)S(1)} %dynamic-update-slice.38, f32[8]{0:T(128)S(1)} %dynamic-update-slice.42), channel_id=1, replica_groups=mesh['lat'=8,'lon_0'=4,'lon_1'=4,'obs'=2] {'lat'}, use_global_device_ids=true, to_apply=%add.32 | all-reduce | flops 16 | bytes 128
  640.4 10.9 %all-reduce.45 = (f32[4]{0:T(128)S(1)}, f32[4]{0:T(128)S(1)}) all-reduce(f32[4]{0:T(128)S(1)} %dynamic-update-slice.40, f32[4]{0:T(128)S(1)} %dynamic-update-slice.44), channel_id=1, replica_groups=mesh['lat'=8,'lon_0'=4,'lon_1'=4,'obs'=2] {'lon_1'}, use_global_device_ids=true, to_apply=%add.34 | all-reduce | flops 8 | bytes 64
  655.2 8.6 %all-reduce.55 = (f32[2]{0:T(128)S(1)}, f32[2]{0:T(128)S(1)}) all-reduce(f32[2]{0:T(128)S(1)} %dynamic-update-slice.41, f32[2]{0:T(128)S(1)} %dynamic-update-slice.45), channel_id=1, replica_groups=mesh['lat'=8,'lon_0'=4,'lon_1'=4,'obs'=2] {'obs'}, use_global_device_ids=true, to_apply=%add.35 | all-reduce | flops 4 | bytes 32
  (319 shorter events, 205.5 us)
Async XLA Ops:
  0.6 20.6 %copy-start.4 = (f32[128,128]{1,0:T(8,128)S(1)}, f32[128,128]{1,0:T(8,128)}, u32[]{:S(2)}) copy-start(f32[128,128]{1,0:T(8,128)} %param.15) | copy-start | bytes 196612
  0.7 20.6 %copy-start.5 = (f32[128,128]{1,0:T(8,128)S(1)}, f32[128,128]{1,0:T(8,128)}, u32[]{:S(2)}) copy-start(f32[128,128]{1,0:T(8,128)} %param.16) | copy-start | bytes 196612
  4.8 28.3 %all-to-all-start = ((s32[128,1,1,3,128]{4,2,3,1,0:T(1,128)}), s32[128,1,1,3,128]{4,2,3,1,0:T(1,128)S(1)}, u32[]{:S(2)}, u32[]{:S(2)}) async-start(s32[128,1,1,3,128]{4,2,3,1,0:T(1,128)} %bitcast.5), calls=%async_computation | async-start | bytes 393216 | tf_op jit(solution)/shard_map/all_to_all | solution.py:51
  33.1 26.9 %all-to-all-start.1 = ((f32[128,1,1,3,3,128]{5,2,4,3,1,0:T(1,128)}), f32[128,1,1,3,3,128]{5,2,4,3,1,0:T(1,128)S(1)}, u32[]{:S(2)}, u32[]{:S(2)}) async-start(f32[128,1,1,3,3,128]{5,2,4,3,1,0:T(1,128)} %copy.29), calls=%async_computation.1 | async-start | bytes 1179648 | tf_op jit(solution)/shard_map/all_to_all | solution.py:51
  289.3 5.8 collective-permute-start
  296.1 3.4 collective-permute-start.1
  308.7 37.2 %copy-start.7 = (u32[256]{0:T(256)S(1)}, u32[256]{0:T(256)}, u32[]{:S(2)}) copy-start(u32[256]{0:T(256)} %constant.158) | copy-start | bytes 3076
  308.7 47.6 %copy-start.6 = (u32[256]{0:T(256)S(1)}, u32[256]{0:T(256)}, u32[]{:S(2)}) copy-start(u32[256]{0:T(256)} %constant.163) | copy-start | bytes 3076
  308.8 4.0 collective-permute-start.2
  311.0 3.0 collective-permute-start.3
  311.1 7.9 %collective-permute-start.6 = (f32[1,1024]{1,0:T(1,128)S(1)}, f32[1,1024]{1,0:T(1,128)S(1)}, u32[]{:S(2)}, u32[]{:S(2)}) collective-permute-start(f32[1,1024]{1,0:T(1,128)S(1)} %get-tuple-element.291), channel_id=1, source_target_pairs={{0,1},{1,32},{32,33},{33,64},{64,65},{65,96},{96,97},{97,128},{128... | collective-permute-start | bytes 12296 | tf_op jit(solution)/shard_map/ppermute | solution.py:19
  312.8 6.2 collective-permute-start.7
  314.2 9.7 %collective-permute-start.4 = (f32[34,1]{1,0:T(8,128)S(1)}, f32[34,1]{1,0:T(8,128)S(1)}, u32[]{:S(2)}, u32[]{:S(2)}) collective-permute-start(f32[34,1]{1,0:T(8,128)S(1)} %get-tuple-element.273), channel_id=1, source_target_pairs={{0,2},{2,4},{4,6},{6,8},{8,10},{10,12},{12,14},{14,16},{16,18},{18... | collective-permute-start | bytes 416 | tf_op jit(solution)/shard_map/ppermute | solution.py:19
  314.2 9.7 %collective-permute-start.5 = (f32[34,1]{1,0:T(8,128)S(1)}, f32[34,1]{1,0:T(8,128)S(1)}, u32[]{:S(2)}, u32[]{:S(2)}) collective-permute-start(f32[34,1]{1,0:T(8,128)S(1)} %get-tuple-element.274), channel_id=1, source_target_pairs={{2,0},{4,2},{6,4},{8,6},{10,8},{12,10},{14,12},{16,14},{18,16},{20... | collective-permute-start | bytes 416 | tf_op jit(solution)/shard_map/ppermute | solution.py:22
  319.0 6.0 collective-permute-start.8
  319.1 5.9 collective-permute-start.9
  385.3 2.7 collective-permute-start.10
  387.3 3.0 collective-permute-start.11
  390.4 6.4 collective-permute-start.12
  390.4 6.4 collective-permute-start.13
  456.8 1.9 collective-permute-start.14
  458.0 3.0 collective-permute-start.15
  461.1 6.0 collective-permute-start.16
  461.2 5.9 collective-permute-start.17
  527.4 2.7 collective-permute-start.18
  529.3 3.0 collective-permute-start.19
  532.4 6.3 collective-permute-start.20
  532.5 6.3 collective-permute-start.21
  598.7 2.0 collective-permute-start.22
  600.0 3.0 collective-permute-start.23
  603.1 6.0 collective-permute-start.24
  603.2 5.9 collective-permute-start.25
  (6 other events, 91.1 us)
